TPU v7x, 1024 devices: a whole 8x8x8 slice. The times are simulated.
1024 devices in a mesh: gx: 64 (over x, z), gy: 16 (over y, core).
Axes of the slice: x: 8, y: 8, z: 8, core: 2. Of those that a mesh axis runs over, the one named last changes fastest.
Arguments:
- species: float32 [53, 256, 128, 128], P(None, 'gx', 'gy'), may hold values from -6 to 6
- diffusion: float32 [53], replicated, may hold values from 0.02 to 0.15
- class_rate: float32 [4], replicated, may hold values from 0.2 to 1
- mixing: float32 [53, 53], replicated, may hold values from -0.3 to 0.3
- inverses: float32 [4, 53, 53], replicated, may hold values from -0.01 to 0.12
- newton_counts: int32 [4], replicated, may hold values from 1 to 8, as said below
- cell_class: int32 [256, 128, 128], P('gx', 'gy'), may hold values from 0 to 3
Outputs:
- updated: float32 [53, 256, 128, 128], P(None, 'gx', 'gy')
Inputs may be any that keep to these rules, and one draw needn't show every extreme that they name: `newton_counts`: nondecreasing in the class; the last class takes 8.
All inputs are finite; a program needn't handle non-finite values.
Results may differ from a plain program's by a relative error of at most 0.0003.
Values sent between devices are 32-bit elements; how exact they have to be, the bound alone decides.
A program may use at most 32 MiB of HBM per device.

v0:
```python
import functools

import jax
import jax.numpy as jnp
from jax import lax
from jax.experimental import pallas as pl
from jax.experimental.pallas import tpu as pltpu
from jax.sharding import PartitionSpec as P

SPEC = 53
PAD = 56
NCLASS = 4
NMAX = 8
F32, BF16 = jnp.float32, jnp.bfloat16
MESH = pl.DeviceIdType.MESH

LAG = 4


def parts_of(v):
    v = jnp.concatenate([v, jnp.zeros((8, v.shape[1]), F32)], axis=0)
    high = v.astype(BF16)
    return high, (v - high.astype(F32)).astype(BF16)


def halves_of(w):
    high = w.astype(BF16).astype(F32)
    return high, w - high


def pick(out, which):
    return jnp.where(
        which == 0,
        out[0:PAD],
        jnp.where(
            which == 1,
            out[PAD : 2 * PAD],
            jnp.where(which == 2, out[2 * PAD : 3 * PAD], out[3 * PAD :]),
        ),
    )


def newton(units, state, drift, cell_count, classes, wstep, wdrift):
    def finish_unit(unit, out, fn):
        for lane, (x, y) in enumerate(unit):
            which = jnp.broadcast_to(classes[x, y : y + 1, :], (PAD, 128))
            fn(x, y, pick(out[:, lane * 128 : (lane + 1) * 128], which))

    def values(unit):
        return jnp.concatenate([state[x + 1, y + 1] for x, y in unit], axis=1)

    def set_drift(x, y, value):
        drift[x * 8 + y] = value

    for unit in units:
        high, low = parts_of(values(unit))
        rhs = jnp.concatenate([high, low, high], axis=0)
        finish_unit(unit, jnp.dot(wdrift[:, :192], rhs, preferred_element_type=F32), set_drift)

    count = len(units)
    steps = count * NMAX
    moved = {}
    for i in range(steps + LAG):
        j = i - LAG
        if 0 <= j < steps:

            def move(x, y, value, k=j // count):
                active = jnp.broadcast_to(cell_count[x, y : y + 1, :] > k, (PAD, 128))
                change = jnp.where(active, value + drift[x * 8 + y], 0.0)
                state[x + 1, y + 1] = state[x + 1, y + 1] + change

            finish_unit(units[j % count], moved.pop(j), move)
        if i < steps:
            now = values(units[i % count])
            t_high, t_low = parts_of(jnp.tanh(now))
            y_high, y_low = parts_of(now)
            rhs = jnp.concatenate([t_high, t_low, y_high, y_low, t_high, y_high], axis=0)
            moved[i] = jnp.dot(wstep[...], rhs, preferred_element_type=F32)


def kernel(
    peers_x, peers_y,
    rate_in, counts_in, diffusion_in, species_in, mixing_in, inverses_in, classes_in,
    out,
    species, mixing, inverses, classes, rate, counts, diffusion,
    grid, state, forcing, drift, cell_count, diff, mix_pad, inv_pad, wstep, wdrift,
    loaded, send, recv,
):
    gx, gy = lax.axis_index("gx"), lax.axis_index("gy")
    sides = (
        ("gx", gx, gx > 0, -1),
        ("gx", gx, gx < peers_x - 1, 1),
        ("gy", gy, gy > 0, -1),
        ("gy", gy, gy < peers_y - 1, 1),
    )

    barrier = pltpu.get_barrier_semaphore()
    for axis, index, there, step in sides:
        @pl.when(there)
        def _(axis=axis, index=index, step=step):
            pl.semaphore_signal(barrier, inc=1, device_id={axis: index + step}, device_id_type=MESH)

    loads = [
        pltpu.make_async_copy(species_in.at[:, x], species.at[:, x], loaded.at[x]) for x in range(4)
    ] + [
        pltpu.make_async_copy(src, dst, loaded.at[4 + i])
        for i, (src, dst) in enumerate((
            (mixing_in, mixing), (inverses_in, inverses), (classes_in, classes),
            (rate_in, rate), (counts_in, counts), (diffusion_in, diffusion),
        ))
    ]
    for i in (0, 3, 1, 2, 4, 5, 6, 7, 8, 9):
        loads[i].start()

    def halo(buffer, side, part):
        return (
            buffer.at[0, pl.ds(1 + 4 * part, 4)],
            buffer.at[5, pl.ds(1 + 4 * part, 4)],
            buffer.at[pl.ds(1, 4), 0],
            buffer.at[pl.ds(1, 4), 9],
        )[side]

    def face(buffer, side, part):
        return (
            buffer.at[1, pl.ds(1 + 4 * part, 4)],
            buffer.at[4, pl.ds(1 + 4 * part, 4)],
            buffer.at[pl.ds(1, 4), 1],
            buffer.at[pl.ds(1, 4), 8],
        )[side]

    parts = (2, 2, 1, 1)
    for side in range(4):
        @pl.when(jnp.logical_not(sides[side][2]))
        def _(side=side):
            for buffer in (grid, state):
                for part in range(parts[side]):
                    edge = halo(buffer, side, part)
                    edge[...] = jnp.zeros(edge.shape, F32)

    def copy(buffer, round_, side, part):
        axis, index, there, step = sides[side]
        return pltpu.make_async_remote_copy(
            src_ref=face(buffer, side, part),
            dst_ref=halo(buffer, side ^ 1, part),
            send_sem=send.at[round_, side, part],
            recv_sem=recv.at[round_, side ^ 1, part],
            device_id={axis: index + step},
            device_id_type=MESH,
        )

    def start(buffer, round_, side, part=0):
        @pl.when(sides[side][2])
        def _():
            copy(buffer, round_, side, part).start()

    def arrived(buffer, round_, side, part=0):
        axis, index, there, step = sides[side]

        @pl.when(there)
        def _():
            pltpu.make_async_remote_copy(
                src_ref=face(buffer, side ^ 1, part),
                dst_ref=halo(buffer, side, part),
                send_sem=send.at[round_, side ^ 1, part],
                recv_sem=recv.at[round_, side, part],
                device_id={axis: index + step},
                device_id_type=MESH,
            ).wait_recv()

    def sent(buffer, round_, side, part=0):
        @pl.when(sides[side][2])
        def _():
            copy(buffer, round_, side, part).wait_send()

    def turn_in(x):
        loads[x].wait()
        for g in range(7):
            rows = min(8, SPEC - 8 * g)
            block = species[8 * g : 8 * g + rows, x]
            if rows < 8:
                block = jnp.concatenate([block, jnp.zeros((8 - rows, 8, 128), F32)], axis=0)
            grid[x + 1, 1:9, 8 * g : 8 * g + 8, :] = jnp.swapaxes(block, 0, 1)

    turn_in(0)
    turn_in(3)
    pl.semaphore_wait(barrier, sum(there.astype(jnp.int32) for _, _, there, _ in sides))
    for side in (0, 1):
        start(grid, 0, side, 0)
    for side in (0, 1):
        start(grid, 0, side, 1)
    turn_in(1)
    turn_in(2)
    for side in (2, 3):
        start(grid, 0, side)
    for i in range(4, 10):
        loads[i].wait()

    mix_pad[...] = jnp.zeros_like(mix_pad)
    mix_pad[0:SPEC, 0:SPEC] = mixing[...]
    inv_pad[...] = jnp.zeros_like(inv_pad)
    for c in range(NCLASS):
        inv_pad[c * PAD : c * PAD + SPEC, 0:SPEC] = inverses[:, c, :]
    product = jnp.dot(
        inv_pad[...], mix_pad[...], precision=lax.Precision.HIGHEST, preferred_element_type=F32
    )
    for c in range(NCLASS):
        rows = slice(c * PAD, (c + 1) * PAD)
        i_high, i_low = halves_of(inv_pad[rows])
        p_high, p_low = halves_of(rate[c] * product[rows])
        q_high, q_low = halves_of((-1.0 - rate[c]) * inv_pad[rows])
        wdrift[rows, 0:128] = (i_high + pltpu.roll(i_high, 64, 1)).astype(BF16)
        wdrift[rows, 128:256] = i_low.astype(BF16)
        wstep[rows, 0:128] = (p_high + pltpu.roll(p_high, 64, 1)).astype(BF16)
        wstep[rows, 128:256] = (q_high + pltpu.roll(q_high, 64, 1)).astype(BF16)
        wstep[rows, 256:384] = (p_low + pltpu.roll(q_low, 64, 1)).astype(BF16)
    diff[...] = jnp.zeros_like(diff)
    for s in range(SPEC):
        diff[s : s + 1, :] = jnp.full((1, 128), diffusion[s], F32)
    cls = classes[...]
    cell_count[...] = jnp.where(
        cls == 0, counts[0], jnp.where(cls == 1, counts[1], jnp.where(cls == 2, counts[2], counts[3]))
    )

    lane = lax.broadcasted_iota(jnp.int32, (PAD, 128), 1)

    def laplace(buffer, x, y):
        here = buffer[x + 1, y + 1]
        total = buffer[x + 2, y + 1] + buffer[x, y + 1]
        total = total + buffer[x + 1, y + 2] + buffer[x + 1, y]
        total = total + jnp.where(lane == 127, 0.0, pltpu.roll(here, 127, 1))
        total = total + jnp.where(lane == 0, 0.0, pltpu.roll(here, 1, 1))
        return total - 6.0 * here, here

    def make_target(x, y):
        lap, here = laplace(grid, x, y)
        force = diff[...] * lap
        target = here + force
        forcing[x * 8 + y] = force
        state[x + 1, y + 1] = target

    def finish(x, y):
        lap, here = laplace(state, x, y)
        forcing[x * 8 + y] = here + 0.5 * (diff[...] * lap - forcing[x * 8 + y])

    def turn_out(x):
        for g in range(7):
            rows = min(8, SPEC - 8 * g)
            block = jnp.swapaxes(forcing[x * 8 : x * 8 + 8, 8 * g : 8 * g + 8, :], 0, 1)
            out[8 * g : 8 * g + rows, x] = block[0:rows]

    def over(first, last, xs, fn):
        for y in range(first, last):
            for x in xs:
                fn(x, y)

    def solve(xs, ys):
        units = [[(x, y), (x, y + 1)] for y in ys for x in xs]
        newton(units, state, drift, cell_count, classes, wstep, wdrift)

    def solve_edge_rows():
        over(0, 2, (1, 2), make_target)
        over(6, 8, (1, 2), make_target)
        solve((1, 2), (0, 6))

    over(2, 6, (1, 2), make_target)
    solve((1, 2), (2, 4))
    for side in (2, 3):
        arrived(grid, 0, side)
    last = lax.rem(gx, 8) == 7
    pl.when(jnp.logical_not(last))(solve_edge_rows)
    for part in range(2):
        for side in (1, 0):
            arrived(grid, 0, side, part)
        over(4 * part, 4 * part + 4, (0, 3), make_target)
        solve((0, 3), (4 * part, 4 * part + 2))
        for side in (1, 0):
            start(state, 1, side, part)
    pl.when(last)(solve_edge_rows)
    for side in (2, 3):
        start(state, 1, side)

    over(1, 7, (1, 2), finish)
    for side in (2, 3):
        arrived(state, 1, side)
    over(0, 1, (1, 2), finish)
    over(7, 8, (1, 2), finish)
    turn_out(1)
    turn_out(2)
    for x, side in ((3, 1), (0, 0)):
        for part in range(2):
            arrived(state, 1, side, part)
            over(4 * part, 4 * part + 4, (x,), finish)
        turn_out(x)
    for round_, buffer in ((0, grid), (1, state)):
        for side in range(4):
            for part in range(parts[side]):
                sent(buffer, round_, side, part)


def solution(mesh):
    peers_x, peers_y = mesh.shape["gx"], mesh.shape["gy"]

    def local(species, diffusion, class_rate, mixing, inverses, newton_counts, cell_class):
        hbm = pl.BlockSpec(memory_space=pltpu.HBM)
        operands = (
            class_rate, newton_counts, diffusion, species, mixing,
            jnp.transpose(inverses, (1, 0, 2)), cell_class,
        )
        return pl.pallas_call(
            functools.partial(kernel, peers_x, peers_y),
            out_shape=jax.ShapeDtypeStruct(species.shape, F32),
            in_specs=[hbm] * 7,
            out_specs=pl.BlockSpec(memory_space=pltpu.VMEM),
            scratch_shapes=[
                pltpu.VMEM((SPEC, 4, 8, 128), F32),
                pltpu.VMEM((SPEC, SPEC), F32),
                pltpu.VMEM((SPEC, NCLASS, SPEC), F32),
                pltpu.VMEM((4, 8, 128), jnp.int32),
                pltpu.SMEM((NCLASS,), F32),
                pltpu.SMEM((NCLASS,), jnp.int32),
                pltpu.SMEM((SPEC,), F32),
                pltpu.VMEM((6, 10, PAD, 128), F32),
                pltpu.VMEM((6, 10, PAD, 128), F32),
                pltpu.VMEM((32, PAD, 128), F32),
                pltpu.VMEM((32, PAD, 128), F32),
                pltpu.VMEM((4, 8, 128), jnp.int32),
                pltpu.VMEM((PAD, 128), F32),
                pltpu.VMEM((128, 128), F32),
                pltpu.VMEM((NCLASS * PAD, 128), F32),
                pltpu.VMEM((NCLASS * PAD, 384), BF16),
                pltpu.VMEM((NCLASS * PAD, 256), BF16),
                pltpu.SemaphoreType.DMA((10,)),
                pltpu.SemaphoreType.DMA((2, 4, 2)),
                pltpu.SemaphoreType.DMA((2, 4, 2)),
            ],
            compiler_params=pltpu.CompilerParams(
                collective_id=0, has_side_effects=True, vmem_limit_bytes=48 * 1024 * 1024
            ),
            name="section",
        )(*(pltpu.with_memory_space_constraint(v, pltpu.HBM) for v in operands))

    in_specs = (P(None, "gx", "gy", None), P(), P(), P(), P(), P(), P("gx", "gy", None))
    out_specs = P(None, "gx", "gy", None)
    return jax.shard_map(local, mesh=mesh, in_specs=in_specs, out_specs=out_specs, check_vma=False)
```

profile of v0, /device:TPU:63, one launch (start us, length us, event | category | flops | bytes accessed | tf_op | source)
XLA Modules:
  0.0 36.9 jit_solution(6897567198485855954)
XLA Ops:
  0.0 36.0 %section.1 = f32[53,4,8,128]{3,2,1,0:T(8,128)S(1)} custom-call(f32[4]{0:T(128)} %rate_in.1, s32[4]{0:T(128)} %counts_in.1, f32[53]{0:T(128)} %diffusion_in.1, f32[53,4,8,128]{3,2,1,0:T(8,128)} %species_in.1, f32[53,53]{1,0:T(8,128)} %mixing_in.1, f32[53,4,53]{2,1,0:T(4,128)} %bitcast.1, s32[4,8,128]{2,1,0:T(8,128)} %classes_in.1), custom_call_target="tpu_custom_call" | custom-call | tf_op jit(solution)/shard_map/section/pallas_call | solution.py:309
  36.0 0.9 %copy.9 = f32[53,4,8,128]{3,2,1,0:T(8,128)} copy(f32[53,4,8,128]{3,2,1,0:T(8,128)S(1)} %section.1) | data formatting | bytes 1736704
where the time goes:
time: 37.1 us; the launch traced here: 36.9 us
  Pallas kernels  36 us (97%)
  local copies, waits for them, and re-layouts  0.91 us (2%)
    pallas_call x1, Pallas kernels, local(): pl.pallas_call(functools.partial(kernel, peers_x, peers_y), out_shape=jax...  36 us
    unnamed x1, local copies, waits for them, and re-layouts  0.91 us

commit v1 on v0

--- a/solution.py
+++ b/solution.py
@@ -94,6 +94,9 @@
         ("gy", gy, gy < peers_y - 1, 1),
     )
 
+    for x in (0, 5):
+        grid[x, 1:9, SPEC:PAD, :] = jnp.zeros((8, PAD - SPEC, 128), F32)
+        state[x, 1:9, SPEC:PAD, :] = jnp.zeros((8, PAD - SPEC, 128), F32)
     barrier = pltpu.get_barrier_semaphore()
     for axis, index, there, step in sides:
         @pl.when(there)
@@ -114,16 +117,16 @@
 
     def halo(buffer, side, part):
         return (
-            buffer.at[0, pl.ds(1 + 4 * part, 4)],
-            buffer.at[5, pl.ds(1 + 4 * part, 4)],
+            buffer.at[0, pl.ds(1 + 4 * part, 4), pl.ds(0, SPEC)],
+            buffer.at[5, pl.ds(1 + 4 * part, 4), pl.ds(0, SPEC)],
             buffer.at[pl.ds(1, 4), 0],
             buffer.at[pl.ds(1, 4), 9],
         )[side]
 
     def face(buffer, side, part):
         return (
-            buffer.at[1, pl.ds(1 + 4 * part, 4)],
-            buffer.at[4, pl.ds(1 + 4 * part, 4)],
+            buffer.at[1, pl.ds(1 + 4 * part, 4), pl.ds(0, SPEC)],
+            buffer.at[4, pl.ds(1 + 4 * part, 4), pl.ds(0, SPEC)],
             buffer.at[pl.ds(1, 4), 1],
             buffer.at[pl.ds(1, 4), 8],
         )[side]

time: 37.1 us -> 37.1 us (level)
  no operation moved by 1% of the time
where the time goes in v1:
time: 37.1 us; the launch traced here: 36.9 us
  Pallas kernels  36 us (97%)
  local copies, waits for them, and re-layouts  0.91 us (2%)
    pallas_call x1, Pallas kernels, local(): pl.pallas_call(functools.partial(kernel, peers_x, peers_y), out_shape=jax...  36 us
    unnamed x1, local copies, waits for them, and re-layouts  0.91 us

profile of v1, /device:TPU:63, one launch (start us, length us, event | category | flops | bytes accessed | tf_op | source)
XLA Modules:
  0.0 36.9 jit_solution(12468647270416895766)
XLA Ops:
  0.0 36.0 %section.1 = f32[53,4,8,128]{3,2,1,0:T(8,128)S(1)} custom-call(f32[4]{0:T(128)} %rate_in.1, s32[4]{0:T(128)} %counts_in.1, f32[53]{0:T(128)} %diffusion_in.1, f32[53,4,8,128]{3,2,1,0:T(8,128)} %species_in.1, f32[53,53]{1,0:T(8,128)} %mixing_in.1, f32[53,4,53]{2,1,0:T(4,128)} %bitcast.1, s32[4,8,128]{2,1,0:T(8,128)} %classes_in.1), custom_call_target="tpu_custom_call" | custom-call | tf_op jit(solution)/shard_map/section/pallas_call | solution.py:312
  36.0 0.9 %copy.9 = f32[53,4,8,128]{3,2,1,0:T(8,128)} copy(f32[53,4,8,128]{3,2,1,0:T(8,128)S(1)} %section.1) | data formatting | bytes 1736704
